TPU v7x, 32 devices: a whole 2x2x4 slice. The times are simulated.
32 devices in a mesh: gx: 4 (over z), gy: 4 (over x, core), gz: 2 (over y).
Axes of the slice: x: 2, y: 2, z: 4, core: 2. Of those that a mesh axis runs over, the one named last changes fastest.
Arguments:
- populations: float32 [19, 16, 32, 512], P(None, 'gz', 'gx', 'gy'), may hold values from 0 to 1, as said below
- omega: float32 [16, 32, 512], P('gz', 'gx', 'gy'), may hold values from 0.8 to 1.7
- obstacle: int32 [16, 32, 512], P('gz', 'gx', 'gy'), may hold values 0 or 1
Outputs:
- lifted: float32 [19, 16, 32, 512], P(None, 'gz', 'gx', 'gy')
- diagnostics: float32 [5], replicated
Inputs may be any that keep to these rules, and one draw needn't show every extreme that they name: `populations`: every population lies between 0.3 and 1.7 times its lattice weight.
All inputs are finite; a program needn't handle non-finite values. No bound on the sum of `obstacle` on one device may be relied on, other than what follows from the above.
Results may differ from a plain program's by a relative error of at most 0.0001.
Values sent between devices are 32-bit elements; how exact they have to be, the bound alone decides.
A program may use at most 128 MiB of HBM per device.

v0:
```python
import jax
import jax.numpy as jnp
from jax import lax
from jax.sharding import PartitionSpec as P

STEPS = 4
JUMP = 2


lattice = [
    (0, 0, 0),
    (1, 0, 0),
    (-1, 0, 0),
    (0, 1, 0),
    (0, -1, 0),
    (0, 0, 1),
    (0, 0, -1),
    (1, 1, 0),
    (-1, -1, 0),
    (1, -1, 0),
    (-1, 1, 0),
    (1, 0, 1),
    (-1, 0, -1),
    (1, 0, -1),
    (-1, 0, 1),
    (0, 1, 1),
    (0, -1, -1),
    (0, 1, -1),
    (0, -1, 1),
]
weights = [1.0 / 3.0] + [1.0 / 18.0] * 6 + [1.0 / 36.0] * 12
opposite = [0, 2, 1, 4, 3, 6, 5, 8, 7, 10, 9, 12, 11, 14, 13, 16, 15, 18, 17]
limiter = 25.0


def extended(x, sides, width):
    for axis, dim in sides:
        size, length = (lax.axis_size(axis), x.shape[dim])
        up = [(i, (i + 1) % size) for i in range(size)]
        down = [(j, i) for i, j in up]
        last = lax.slice_in_dim(x, length - width, length, axis=dim)
        first = lax.slice_in_dim(x, 0, width, axis=dim)
        before = lax.ppermute(last, axis, up)
        after = lax.ppermute(first, axis, down)
        x = jnp.concatenate([before, x, after], axis=dim)
    return x


def moments(f):
    rho = jnp.sum(f, axis=0)
    comps = []
    for axis_pick in range(3):
        total = jnp.zeros_like(rho)
        for index in range(19):
            comp = lattice[index][axis_pick]
            if comp != 0:
                total = total + comp * f[index]
        comps.append(total)
    return (rho, comps[0], comps[1], comps[2])


def equilibrium(rho, momx, momy, momz):
    safe = jnp.maximum(rho, 0.5)
    velx, vely, velz = (momx / safe, momy / safe, momz / safe)
    square = velx * velx + vely * vely + velz * velz
    rows = []
    for index in range(19):
        cx, cy, cz = lattice[index]
        proj = cx * velx + cy * vely + cz * velz
        rows.append(weights[index] * rho * (1.0 + 3.0 * proj + 4.5 * proj * proj - 1.5 * square))
    return jnp.stack(rows, 0)


def collide(f, omega, solid):
    rho, momx, momy, momz = moments(f)
    feq = equilibrium(rho, momx, momy, momz)
    post = f + omega[None] * (feq - f)
    flipped = jnp.stack([f[opposite[index]] for index in range(19)], 0)
    return jnp.where(solid[None], flipped, post)


def stream(padded):
    size_z = padded.shape[1] - 2
    size_x = padded.shape[2] - 2
    size_y = padded.shape[3] - 2
    rows = []
    for index in range(19):
        cx, cy, cz = lattice[index]
        rows.append(
            padded[
                index, 1 - cz : 1 - cz + size_z, 1 - cx : 1 - cx + size_x, 1 - cy : 1 - cy + size_y
            ]
        )
    return jnp.stack(rows, 0)


def per_device(populations, omega, obstacle):
    solid = obstacle == 1
    f = populations
    before = f
    for step in range(STEPS):
        post = collide(f, omega, solid)
        padded = extended(post, (("gx", 2), ("gy", 3), ("gz", 1)), 1)
        f = stream(padded)
        if step == STEPS - 2:
            before = f
    rho_a, jxa, jya, jza = moments(before)
    rho_b, jxb, jyb, jzb = moments(f)
    cells = float(
        f.shape[1]
        * f.shape[2]
        * f.shape[3]
        * lax.axis_size("gx")
        * lax.axis_size("gy")
        * lax.axis_size("gz")
    )
    diff_rho = rho_b - rho_a
    diff_x = jxb - jxa
    diff_y = jyb - jya
    diff_z = jzb - jza
    local_terms = (
        jnp.sum(diff_rho * diff_rho),
        jnp.sum(diff_x * diff_x + diff_y * diff_y + diff_z * diff_z),
        jnp.sum(jxb),
        jnp.sum(jyb),
        jnp.sum(jzb),
        jnp.sum(diff_x),
        jnp.sum(diff_y),
        jnp.sum(diff_z),
        jnp.sum(jxb * jxb + jyb * jyb + jzb * jzb),
        jnp.sum(jxb * diff_x + jyb * diff_y + jzb * diff_z),
    )
    (
        change_rho,
        change_mom,
        base_x,
        base_y,
        base_z,
        delta_x,
        delta_y,
        delta_z,
        energy_base,
        energy_cross,
    ) = lax.psum(
        (
            local_terms[0],
            local_terms[1],
            local_terms[2],
            local_terms[3],
            local_terms[4],
            local_terms[5],
            local_terms[6],
            local_terms[7],
            local_terms[8],
            local_terms[9],
        ),
        ("gx", "gy", "gz"),
    )
    change = (change_rho + change_mom) / cells
    gain = JUMP / (1.0 + limiter * change)
    jxp = jxb + gain * diff_x
    jyp = jyb + gain * diff_y
    jzp = jzb + gain * diff_z
    sum_x = base_x + gain * delta_x
    sum_y = base_y + gain * delta_y
    sum_z = base_z + gain * delta_z
    energy = energy_base + 2.0 * gain * energy_cross + gain * gain * change_mom
    rho_p = rho_b + gain * diff_rho
    lifted = equilibrium(rho_p, jxp, jyp, jzp)
    diagnostics = jnp.stack([change, sum_x / cells, sum_y / cells, sum_z / cells, energy / cells])
    return (lifted, diagnostics)


def solution(mesh):
    in_specs = (P(None, "gz", "gx", "gy"), P("gz", "gx", "gy"), P("gz", "gx", "gy"))
    out_specs = (P(None, "gz", "gx", "gy"), P())
    return jax.shard_map(
        per_device, mesh=mesh, in_specs=in_specs, out_specs=out_specs, check_vma=False
    )
```

profile of v0, /device:TPU:0, one launch (start us, length us, event | category | flops | bytes accessed | tf_op | source)
XLA Modules:
  0.0 191.6 jit_solution(2588128891063399128)
XLA Ops:
  0.6 0.8 constant_dynamic-update-slice_fusion.18
  1.4 1.1 reduce_sum.2193
  2.5 1.1 constant_dynamic-update-slice_fusion.37
  5.4 5.1 %collective-permute-start = (f32[19,8,1,128]{3,2,1,0:T(1,128)S(1)}, f32[19,8,1,128]{3,2,1,0:T(1,128)S(1)}, u32[]{:S(2)}, u32[]{:S(2)}) collective-permute-start(f32[19,8,1,128]{3,2,1,0:T(1,128)S(1)} %get-tuple-element.152), channel_id=1, source_target_pairs={{8,0},{16,8},{24,16},{0,24},{9,1},{17,9},{25,17},{1,25},{10,2},{18... | collective-permute-start | bytes 233480 | tf_op jit(solution)/shard_map/ppermute | solution.py:44
  10.5 2.4 %collective-permute-done = f32[19,8,1,128]{3,2,1,0:T(1,128)S(1)} collective-permute-done((f32[19,8,1,128]{3,2,1,0:T(1,128)S(1)}, f32[19,8,1,128]{3,2,1,0:T(1,128)S(1)}, u32[]{:S(2)}, u32[]{:S(2)}) %collective-permute-start) | collective-permute-done | bytes 77856 | tf_op jit(solution)/shard_map/ppermute | solution.py:44
  13.0 3.7 %collective-permute-done.1 = f32[19,8,1,128]{3,2,1,0:T(1,128)S(1)} collective-permute-done((f32[19,8,1,128]{3,2,1,0:T(1,128)S(1)}, f32[19,8,1,128]{3,2,1,0:T(1,128)S(1)}, u32[]{:S(2)}, u32[]{:S(2)}) %collective-permute-start.1) | collective-permute-done | bytes 77856 | tf_op jit(solution)/shard_map/ppermute | solution.py:43
  19.8 1.4 copy.201
  21.2 1.1 collective-permute-done.3
  22.3 1.4 copy.203
  24.1 1.6 collective-permute-start.4
  26.3 8.1 %collective-permute-done.4 = f32[19,1,10,130]{3,2,1,0:T(8,128)S(1)} collective-permute-done((f32[19,1,10,130]{3,2,1,0:T(8,128)S(1)}, f32[19,1,10,130]{3,2,1,0:T(8,128)S(1)}, u32[]{:S(2)}, u32[]{:S(2)}) %collective-permute-start.4) | collective-permute-done | bytes 98832 | tf_op jit(solution)/shard_map/ppermute | solution.py:44
  34.4 6.2 %collective-permute-done.5 = f32[19,1,10,130]{3,2,1,0:T(8,128)S(1)} collective-permute-done((f32[19,1,10,130]{3,2,1,0:T(8,128)S(1)}, f32[19,1,10,130]{3,2,1,0:T(8,128)S(1)}, u32[]{:S(2)}, u32[]{:S(2)}) %collective-permute-start.5) | collective-permute-done | bytes 98832 | tf_op jit(solution)/shard_map/ppermute | solution.py:43
  42.8 1.5 collective-permute-start.7
  44.3 2.4 %collective-permute-done.6 = f32[19,8,1,128]{3,2,1,0:T(1,128)S(1)} collective-permute-done((f32[19,8,1,128]{3,2,1,0:T(1,128)S(1)}, f32[19,8,1,128]{3,2,1,0:T(1,128)S(1)}, u32[]{:S(2)}, u32[]{:S(2)}) %collective-permute-start.6) | collective-permute-done | bytes 77856 | tf_op jit(solution)/shard_map/ppermute | solution.py:44
  46.7 2.3 %collective-permute-done.7 = f32[19,8,1,128]{3,2,1,0:T(1,128)S(1)} collective-permute-done((f32[19,8,1,128]{3,2,1,0:T(1,128)S(1)}, f32[19,8,1,128]{3,2,1,0:T(1,128)S(1)}, u32[]{:S(2)}, u32[]{:S(2)}) %collective-permute-start.7) | collective-permute-done | bytes 77856 | tf_op jit(solution)/shard_map/ppermute | solution.py:43
  49.7 0.7 copy.206
  51.1 0.7 collective-permute-start.9
  52.1 1.4 copy.207
  53.5 1.3 collective-permute-done.9
  54.8 1.4 copy.209
  56.6 1.6 collective-permute-start.10
  58.8 8.1 %collective-permute-done.10 = f32[19,1,10,130]{3,2,1,0:T(8,128)S(1)} collective-permute-done((f32[19,1,10,130]{3,2,1,0:T(8,128)S(1)}, f32[19,1,10,130]{3,2,1,0:T(8,128)S(1)}, u32[]{:S(2)}, u32[]{:S(2)}) %collective-permute-start.10) | collective-permute-done | bytes 98832 | tf_op jit(solution)/shard_map/ppermute | solution.py:44
  66.9 5.1 %collective-permute-done.11 = f32[19,1,10,130]{3,2,1,0:T(8,128)S(1)} collective-permute-done((f32[19,1,10,130]{3,2,1,0:T(8,128)S(1)}, f32[19,1,10,130]{3,2,1,0:T(8,128)S(1)}, u32[]{:S(2)}, u32[]{:S(2)}) %collective-permute-start.11) | collective-permute-done | bytes 98832 | tf_op jit(solution)/shard_map/ppermute | solution.py:43
  73.8 1.9 %collective-permute-start.13 = (f32[19,8,1,128]{3,2,1,0:T(1,128)S(1)}, f32[19,8,1,128]{3,2,1,0:T(1,128)S(1)}, u32[]{:S(2)}, u32[]{:S(2)}) collective-permute-start(f32[19,8,1,128]{3,2,1,0:T(1,128)S(1)} %get-tuple-element.147), channel_id=1, source_target_pairs={{0,8},{8,16},{16,24},{24,0},{1,9},{9,17},{17,25},{25,1},{2,10},{10... | collective-permute-start | bytes 233480 | tf_op jit(solution)/shard_map/ppermute | solution.py:43
  75.7 2.7 %collective-permute-done.12 = f32[19,8,1,128]{3,2,1,0:T(1,128)S(1)} collective-permute-done((f32[19,8,1,128]{3,2,1,0:T(1,128)S(1)}, f32[19,8,1,128]{3,2,1,0:T(1,128)S(1)}, u32[]{:S(2)}, u32[]{:S(2)}) %collective-permute-start.12) | collective-permute-done | bytes 77856 | tf_op jit(solution)/shard_map/ppermute | solution.py:44
  78.4 1.5 collective-permute-done.13
  80.6 0.7 copy.212
  83.0 1.4 copy.213
  84.4 1.6 collective-permute-done.15
  86.0 1.4 copy.215
  87.9 1.6 collective-permute-start.16
  90.1 8.1 %collective-permute-done.16 = f32[19,1,10,130]{3,2,1,0:T(8,128)S(1)} collective-permute-done((f32[19,1,10,130]{3,2,1,0:T(8,128)S(1)}, f32[19,1,10,130]{3,2,1,0:T(8,128)S(1)}, u32[]{:S(2)}, u32[]{:S(2)}) %collective-permute-start.16) | collective-permute-done | bytes 98832 | tf_op jit(solution)/shard_map/ppermute | solution.py:44
  98.2 6.4 %collective-permute-done.17 = f32[19,1,10,130]{3,2,1,0:T(8,128)S(1)} collective-permute-done((f32[19,1,10,130]{3,2,1,0:T(8,128)S(1)}, f32[19,1,10,130]{3,2,1,0:T(8,128)S(1)}, u32[]{:S(2)}, u32[]{:S(2)}) %collective-permute-start.17) | collective-permute-done | bytes 98832 | tf_op jit(solution)/shard_map/ppermute | solution.py:43
  106.9 3.8 %collective-permute-start.19 = (f32[19,8,1,128]{3,2,1,0:T(1,128)S(1)}, f32[19,8,1,128]{3,2,1,0:T(1,128)S(1)}, u32[]{:S(2)}, u32[]{:S(2)}) collective-permute-start(f32[19,8,1,128]{3,2,1,0:T(1,128)S(1)} %get-tuple-element.145), channel_id=1, source_target_pairs={{8,0},{16,8},{24,16},{0,24},{9,1},{17,9},{25,17},{1,25},{10,2},{18... | collective-permute-start | bytes 233480 | tf_op jit(solution)/shard_map/ppermute | solution.py:44
  110.7 2.9 %collective-permute-done.18 = f32[19,8,1,128]{3,2,1,0:T(1,128)S(1)} collective-permute-done((f32[19,8,1,128]{3,2,1,0:T(1,128)S(1)}, f32[19,8,1,128]{3,2,1,0:T(1,128)S(1)}, u32[]{:S(2)}, u32[]{:S(2)}) %collective-permute-start.18) | collective-permute-done | bytes 77856 | tf_op jit(solution)/shard_map/ppermute | solution.py:43
  114.2 1.3 copy.218
  116.3 1.8 collective-permute-start.21
  118.0 1.4 collective-permute-done.20
  119.4 1.4 copy.219
  120.8 2.2 %copy.221 = f32[19,8,10,1]{3,2,1,0:T(8,128)S(1)} copy(f32[19,8,10,1]{0,1,3,2:T(8,128)} %collective-permute-done.21) | data formatting | bytes 12160 | tf_op jit(solution)/shard_map/ppermute | solution.py:44
  123.5 1.6 collective-permute-start.22
  125.7 8.1 %collective-permute-done.22 = f32[19,1,10,130]{3,2,1,0:T(8,128)S(1)} collective-permute-done((f32[19,1,10,130]{3,2,1,0:T(8,128)S(1)}, f32[19,1,10,130]{3,2,1,0:T(8,128)S(1)}, u32[]{:S(2)}, u32[]{:S(2)}) %collective-permute-start.22) | collective-permute-done | bytes 98832 | tf_op jit(solution)/shard_map/ppermute | solution.py:43
  133.8 4.5 %collective-permute-done.23 = f32[19,1,10,130]{3,2,1,0:T(8,128)S(1)} collective-permute-done((f32[19,1,10,130]{3,2,1,0:T(8,128)S(1)}, f32[19,1,10,130]{3,2,1,0:T(8,128)S(1)}, u32[]{:S(2)}, u32[]{:S(2)}) %collective-permute-start.23) | collective-permute-done | bytes 98832 | tf_op jit(solution)/shard_map/ppermute | solution.py:44
  139.6 0.7 add_reduce_fusion
  140.4 1.5 fusion.287
  141.9 40.1 %all-reduce = (f32[]{:T(128)}, f32[]{:T(128)}, f32[]{:T(128)}, f32[]{:T(128)}, f32[]{:T(128)}, /*index=5*/f32[]{:T(128)}, f32[]{:T(128)}, f32[]{:T(128)}, f32[]{:T(128)}, f32[]{:T(128)}) all-reduce(f32[]{:T(128)} %fusion.287, f32[]{:T(128)} %get-tuple-element.5, ...), channel_id=1, replica_groups=mesh['gx'=4,'gy'=4,'gz'=2] {'gx','gy','gz'}, use_global_device_ids=true, to_apply=%region_2.3 | all-reduce | flops 10 | bytes 80 | tf_op jit(solution)/shard_map/psum | solution.py:144
  183.4 1.2 constant_dynamic-update-slice_fusion.227
  190.8 0.7 stack.53
  (357 shorter events, 20.7 us)
Async XLA Ops:
  5.4 7.6 %collective-permute-start = (f32[19,8,1,128]{3,2,1,0:T(1,128)S(1)}, f32[19,8,1,128]{3,2,1,0:T(1,128)S(1)}, u32[]{:S(2)}, u32[]{:S(2)}) collective-permute-start(f32[19,8,1,128]{3,2,1,0:T(1,128)S(1)} %get-tuple-element.152), channel_id=1, source_target_pairs={{8,0},{16,8},{24,16},{0,24},{9,1},{17,9},{25,17},{1,25},{10,2},{18... | collective-permute-start | bytes 233480 | tf_op jit(solution)/shard_map/ppermute | solution.py:44
  10.5 6.2 %collective-permute-start.1 = (f32[19,8,1,128]{3,2,1,0:T(1,128)S(1)}, f32[19,8,1,128]{3,2,1,0:T(1,128)S(1)}, u32[]{:S(2)}, u32[]{:S(2)}) collective-permute-start(f32[19,8,1,128]{3,2,1,0:T(1,128)S(1)} %get-tuple-element.151), channel_id=1, source_target_pairs={{0,8},{8,16},{16,24},{24,0},{1,9},{9,17},{17,25},{25,1},{2,10},{10... | collective-permute-start | bytes 233480 | tf_op jit(solution)/shard_map/ppermute | solution.py:43
  18.1 1.7 collective-permute-start.2
  18.8 3.5 %collective-permute-start.3 = (f32[19,8,10,1]{0,1,3,2:T(8,128)S(1)}, f32[19,8,10,1]{0,1,3,2:T(8,128)S(1)}, u32[]{:S(2)}, u32[]{:S(2)}) collective-permute-start(f32[19,8,10,1]{0,1,3,2:T(8,128)S(1)} %copy.202), channel_id=1, source_target_pairs={{0,2},{2,4},{4,6},{6,0},{1,3},{3,5},{5,7},{7,1},{8,10},{10,12},{12... | collective-permute-start | bytes 18248 | tf_op jit(solution)/shard_map/ppermute | solution.py:43
  24.1 10.3 %collective-permute-start.4 = (f32[19,1,10,130]{3,2,1,0:T(8,128)S(1)}, f32[19,1,10,130]{3,2,1,0:T(8,128)S(1)}, u32[]{:S(2)}, u32[]{:S(2)}) collective-permute-start(f32[19,1,10,130]{3,2,1,0:T(8,128)S(1)} %get-tuple-element.136), channel_id=1, source_target_pairs={{1,0},{0,1},{3,2},{2,3},{5,4},{4,5},{7,6},{6,7},{9,8},{8,9},{11,10... | collective-permute-start | bytes 296408 | tf_op jit(solution)/shard_map/ppermute | solution.py:44
  25.7 14.9 %collective-permute-start.5 = (f32[19,1,10,130]{3,2,1,0:T(8,128)S(1)}, f32[19,1,10,130]{3,2,1,0:T(8,128)S(1)}, u32[]{:S(2)}, u32[]{:S(2)}) collective-permute-start(f32[19,1,10,130]{3,2,1,0:T(8,128)S(1)} %get-tuple-element.135), channel_id=1, source_target_pairs={{0,1},{1,0},{2,3},{3,2},{4,5},{5,4},{6,7},{7,6},{8,9},{9,8},{10,11... | collective-permute-start | bytes 296408 | tf_op jit(solution)/shard_map/ppermute | solution.py:43
  42.2 4.5 %collective-permute-start.6 = (f32[19,8,1,128]{3,2,1,0:T(1,128)S(1)}, f32[19,8,1,128]{3,2,1,0:T(1,128)S(1)}, u32[]{:S(2)}, u32[]{:S(2)}) collective-permute-start(f32[19,8,1,128]{3,2,1,0:T(1,128)S(1)} %get-tuple-element.150), channel_id=1, source_target_pairs={{8,0},{16,8},{24,16},{0,24},{9,1},{17,9},{25,17},{1,25},{10,2},{18... | collective-permute-start | bytes 233480 | tf_op jit(solution)/shard_map/ppermute | solution.py:44
  42.8 6.2 %collective-permute-start.7 = (f32[19,8,1,128]{3,2,1,0:T(1,128)S(1)}, f32[19,8,1,128]{3,2,1,0:T(1,128)S(1)}, u32[]{:S(2)}, u32[]{:S(2)}) collective-permute-start(f32[19,8,1,128]{3,2,1,0:T(1,128)S(1)} %get-tuple-element.149), channel_id=1, source_target_pairs={{0,8},{8,16},{16,24},{24,0},{1,9},{9,17},{17,25},{25,1},{2,10},{10... | collective-permute-start | bytes 233480 | tf_op jit(solution)/shard_map/ppermute | solution.py:43
  50.4 1.7 collective-permute-start.8
  51.1 3.6 %collective-permute-start.9 = (f32[19,8,10,1]{0,1,3,2:T(8,128)S(1)}, f32[19,8,10,1]{0,1,3,2:T(8,128)S(1)}, u32[]{:S(2)}, u32[]{:S(2)}) collective-permute-start(f32[19,8,10,1]{0,1,3,2:T(8,128)S(1)} %copy.208), channel_id=1, source_target_pairs={{0,2},{2,4},{4,6},{6,0},{1,3},{3,5},{5,7},{7,1},{8,10},{10,12},{12... | collective-permute-start | bytes 18248 | tf_op jit(solution)/shard_map/ppermute | solution.py:43
  56.6 10.3 %collective-permute-start.10 = (f32[19,1,10,130]{3,2,1,0:T(8,128)S(1)}, f32[19,1,10,130]{3,2,1,0:T(8,128)S(1)}, u32[]{:S(2)}, u32[]{:S(2)}) collective-permute-start(f32[19,1,10,130]{3,2,1,0:T(8,128)S(1)} %get-tuple-element.134), channel_id=1, source_target_pairs={{1,0},{0,1},{3,2},{2,3},{5,4},{4,5},{7,6},{6,7},{9,8},{8,9},{11,10... | collective-permute-start | bytes 296408 | tf_op jit(solution)/shard_map/ppermute | solution.py:44
  58.2 13.8 %collective-permute-start.11 = (f32[19,1,10,130]{3,2,1,0:T(8,128)S(1)}, f32[19,1,10,130]{3,2,1,0:T(8,128)S(1)}, u32[]{:S(2)}, u32[]{:S(2)}) collective-permute-start(f32[19,1,10,130]{3,2,1,0:T(8,128)S(1)} %get-tuple-element.133), channel_id=1, source_target_pairs={{0,1},{1,0},{2,3},{3,2},{4,5},{5,4},{6,7},{7,6},{8,9},{9,8},{10,11... | collective-permute-start | bytes 296408 | tf_op jit(solution)/shard_map/ppermute | solution.py:43
  73.5 31.1 %copy-start = (f32[19,8,8,128]{3,2,1,0:T(8,128)}, f32[19,8,8,128]{3,2,1,0:T(8,128)S(1)}, u32[]{:S(2)}) copy-start(f32[19,8,8,128]{3,2,1,0:T(8,128)S(1)} %add_select_fusion.1) | copy-start | bytes 1867780
  73.6 4.8 %collective-permute-start.12 = (f32[19,8,1,128]{3,2,1,0:T(1,128)S(1)}, f32[19,8,1,128]{3,2,1,0:T(1,128)S(1)}, u32[]{:S(2)}, u32[]{:S(2)}) collective-permute-start(f32[19,8,1,128]{3,2,1,0:T(1,128)S(1)} %get-tuple-element.148), channel_id=1, source_target_pairs={{8,0},{16,8},{24,16},{0,24},{9,1},{17,9},{25,17},{1,25},{10,2},{18... | collective-permute-start | bytes 233480 | tf_op jit(solution)/shard_map/ppermute | solution.py:44
  73.8 6.2 %collective-permute-start.13 = (f32[19,8,1,128]{3,2,1,0:T(1,128)S(1)}, f32[19,8,1,128]{3,2,1,0:T(1,128)S(1)}, u32[]{:S(2)}, u32[]{:S(2)}) collective-permute-start(f32[19,8,1,128]{3,2,1,0:T(1,128)S(1)} %get-tuple-element.147), channel_id=1, source_target_pairs={{0,8},{8,16},{16,24},{24,0},{1,9},{9,17},{17,25},{25,1},{2,10},{10... | collective-permute-start | bytes 233480 | tf_op jit(solution)/shard_map/ppermute | solution.py:43
  78.4 9.0 %copy-start.24 = (f32[19,8,1,128]{3,2,1,0:T(1,128)}, f32[19,8,1,128]{3,2,1,0:T(1,128)S(1)}, u32[]{:S(2)}) copy-start(f32[19,8,1,128]{3,2,1,0:T(1,128)S(1)} %collective-permute-done.12) | copy-start | bytes 233476
  79.9 7.5 %copy-start.26 = (f32[19,8,1,128]{3,2,1,0:T(1,128)}, f32[19,8,1,128]{3,2,1,0:T(1,128)S(1)}, u32[]{:S(2)}) copy-start(f32[19,8,1,128]{3,2,1,0:T(1,128)S(1)} %collective-permute-done.13) | copy-start | bytes 233476
  81.3 1.7 collective-permute-start.14
  82.1 3.9 %collective-permute-start.15 = (f32[19,8,10,1]{0,1,3,2:T(8,128)S(1)}, f32[19,8,10,1]{0,1,3,2:T(8,128)S(1)}, u32[]{:S(2)}, u32[]{:S(2)}) collective-permute-start(f32[19,8,10,1]{0,1,3,2:T(8,128)S(1)} %copy.214), channel_id=1, source_target_pairs={{0,2},{2,4},{4,6},{6,0},{1,3},{3,5},{5,7},{7,1},{8,10},{10,12},{12... | collective-permute-start | bytes 18248 | tf_op jit(solution)/shard_map/ppermute | solution.py:43
  87.9 16.7 %copy-start.25 = (f32[19,8,1,128]{3,2,1,0:T(1,128)S(1)}, f32[19,8,1,128]{3,2,1,0:T(1,128)}, u32[]{:S(2)}) copy-start(f32[19,8,1,128]{3,2,1,0:T(1,128)} %copy-done.24) | copy-start | bytes 233476
  87.9 16.7 %copy-start.27 = (f32[19,8,1,128]{3,2,1,0:T(1,128)S(1)}, f32[19,8,1,128]{3,2,1,0:T(1,128)}, u32[]{:S(2)}) copy-start(f32[19,8,1,128]{3,2,1,0:T(1,128)} %copy-done.26) | copy-start | bytes 233476
  87.9 10.3 %collective-permute-start.16 = (f32[19,1,10,130]{3,2,1,0:T(8,128)S(1)}, f32[19,1,10,130]{3,2,1,0:T(8,128)S(1)}, u32[]{:S(2)}, u32[]{:S(2)}) collective-permute-start(f32[19,1,10,130]{3,2,1,0:T(8,128)S(1)} %get-tuple-element.132), channel_id=1, source_target_pairs={{1,0},{0,1},{3,2},{2,3},{5,4},{4,5},{7,6},{6,7},{9,8},{8,9},{11,10... | collective-permute-start | bytes 296408 | tf_op jit(solution)/shard_map/ppermute | solution.py:44
  89.5 15.1 %collective-permute-start.17 = (f32[19,1,10,130]{3,2,1,0:T(8,128)S(1)}, f32[19,1,10,130]{3,2,1,0:T(8,128)S(1)}, u32[]{:S(2)}, u32[]{:S(2)}) collective-permute-start(f32[19,1,10,130]{3,2,1,0:T(8,128)S(1)} %get-tuple-element.131), channel_id=1, source_target_pairs={{0,1},{1,0},{2,3},{3,2},{4,5},{5,4},{6,7},{7,6},{8,9},{9,8},{10,11... | collective-permute-start | bytes 296408 | tf_op jit(solution)/shard_map/ppermute | solution.py:43
  106.8 6.7 %collective-permute-start.18 = (f32[19,8,1,128]{3,2,1,0:T(1,128)S(1)}, f32[19,8,1,128]{3,2,1,0:T(1,128)S(1)}, u32[]{:S(2)}, u32[]{:S(2)}) collective-permute-start(f32[19,8,1,128]{3,2,1,0:T(1,128)S(1)} %get-tuple-element.146), channel_id=1, source_target_pairs={{0,8},{8,16},{16,24},{24,0},{1,9},{9,17},{17,25},{25,1},{2,10},{10... | collective-permute-start | bytes 233480 | tf_op jit(solution)/shard_map/ppermute | solution.py:43
  106.9 6.7 %collective-permute-start.19 = (f32[19,8,1,128]{3,2,1,0:T(1,128)S(1)}, f32[19,8,1,128]{3,2,1,0:T(1,128)S(1)}, u32[]{:S(2)}, u32[]{:S(2)}) collective-permute-start(f32[19,8,1,128]{3,2,1,0:T(1,128)S(1)} %get-tuple-element.145), channel_id=1, source_target_pairs={{8,0},{16,8},{24,16},{0,24},{9,1},{17,9},{25,17},{1,25},{10,2},{18... | collective-permute-start | bytes 233480 | tf_op jit(solution)/shard_map/ppermute | solution.py:44
  115.6 3.9 %collective-permute-start.20 = (f32[19,8,10,1]{0,1,3,2:T(8,128)}, f32[19,8,10,1]{0,1,3,2:T(8,128)S(1)}, u32[]{:S(2)}, u32[]{:S(2)}) collective-permute-start(f32[19,8,10,1]{0,1,3,2:T(8,128)} %copy.218), channel_id=1, source_target_pairs={{0,2},{2,4},{4,6},{6,0},{1,3},{3,5},{5,7},{7,1},{8,10},{10,12},{12... | collective-permute-start | bytes 18248 | tf_op jit(solution)/shard_map/ppermute | solution.py:43
  116.3 4.5 %collective-permute-start.21 = (f32[19,8,10,1]{0,1,3,2:T(8,128)S(1)}, f32[19,8,10,1]{0,1,3,2:T(8,128)}, u32[]{:S(2)}, u32[]{:S(2)}) collective-permute-start(f32[19,8,10,1]{0,1,3,2:T(8,128)S(1)} %copy.220), channel_id=1, source_target_pairs={{2,0},{4,2},{6,4},{0,6},{3,1},{5,3},{7,5},{1,7},{10,8},{12,10},{14... | collective-permute-start | bytes 18248 | tf_op jit(solution)/shard_map/ppermute | solution.py:44
  122.9 15.3 %copy-start.7 = (f32[1,8,8,128]{3,2,1,0:T(8,128)S(1)}, f32[1,8,8,128]{3,2,1,0:T(8,128)}, u32[]{:S(2)}) copy-start(f32[1,8,8,128]{3,2,1,0:T(8,128)} %copy-done.6) | copy-start | bytes 98308
  122.9 15.3 %copy-start.9 = (f32[1,8,8,128]{3,2,1,0:T(8,128)S(1)}, f32[1,8,8,128]{3,2,1,0:T(8,128)}, u32[]{:S(2)}) copy-start(f32[1,8,8,128]{3,2,1,0:T(8,128)} %copy-done.8) | copy-start | bytes 98308
  123.0 15.3 %copy-start.11 = (f32[1,8,8,128]{3,2,1,0:T(8,128)S(1)}, f32[1,8,8,128]{3,2,1,0:T(8,128)}, u32[]{:S(2)}) copy-start(f32[1,8,8,128]{3,2,1,0:T(8,128)} %copy-done.10) | copy-start | bytes 98308
  123.0 15.3 %copy-start.15 = (f32[1,8,8,128]{3,2,1,0:T(8,128)S(1)}, f32[1,8,8,128]{3,2,1,0:T(8,128)}, u32[]{:S(2)}) copy-start(f32[1,8,8,128]{3,2,1,0:T(8,128)} %copy-done.14) | copy-start | bytes 98308
  123.0 15.3 %copy-start.21 = (f32[1,8,8,128]{3,2,1,0:T(8,128)S(1)}, f32[1,8,8,128]{3,2,1,0:T(8,128)}, u32[]{:S(2)}) copy-start(f32[1,8,8,128]{3,2,1,0:T(8,128)} %copy-done.20) | copy-start | bytes 98308
  123.0 15.3 %copy-start.33 = (f32[1,8,8,128]{3,2,1,0:T(8,128)S(1)}, f32[1,8,8,128]{3,2,1,0:T(8,128)}, u32[]{:S(2)}) copy-start(f32[1,8,8,128]{3,2,1,0:T(8,128)} %copy-done.32) | copy-start | bytes 98308
  123.5 10.3 %collective-permute-start.22 = (f32[19,1,10,130]{3,2,1,0:T(8,128)S(1)}, f32[19,1,10,130]{3,2,1,0:T(8,128)S(1)}, u32[]{:S(2)}, u32[]{:S(2)}) collective-permute-start(f32[19,1,10,130]{3,2,1,0:T(8,128)S(1)} %get-tuple-element.129), channel_id=1, source_target_pairs={{0,1},{1,0},{2,3},{3,2},{4,5},{5,4},{6,7},{7,6},{8,9},{9,8},{10,11... | collective-permute-start | bytes 296408 | tf_op jit(solution)/shard_map/ppermute | solution.py:43
  125.1 13.5 %copy-start.3 = (f32[1,8,8,128]{3,2,1,0:T(8,128)S(1)}, f32[1,8,8,128]{3,2,1,0:T(8,128)}, u32[]{:S(2)}) copy-start(f32[1,8,8,128]{3,2,1,0:T(8,128)} %copy-done.2) | copy-start | bytes 98308
  125.1 13.6 %copy-start.5 = (f32[1,8,8,128]{3,2,1,0:T(8,128)S(1)}, f32[1,8,8,128]{3,2,1,0:T(8,128)}, u32[]{:S(2)}) copy-start(f32[1,8,8,128]{3,2,1,0:T(8,128)} %copy-done.4) | copy-start | bytes 98308
  125.1 13.6 %copy-start.13 = (f32[1,8,8,128]{3,2,1,0:T(8,128)S(1)}, f32[1,8,8,128]{3,2,1,0:T(8,128)}, u32[]{:S(2)}) copy-start(f32[1,8,8,128]{3,2,1,0:T(8,128)} %copy-done.12) | copy-start | bytes 98308
  125.1 13.6 %copy-start.17 = (f32[1,8,8,128]{3,2,1,0:T(8,128)S(1)}, f32[1,8,8,128]{3,2,1,0:T(8,128)}, u32[]{:S(2)}) copy-start(f32[1,8,8,128]{3,2,1,0:T(8,128)} %copy-done.16) | copy-start | bytes 98308
  125.1 13.6 %copy-start.19 = (f32[1,8,8,128]{3,2,1,0:T(8,128)S(1)}, f32[1,8,8,128]{3,2,1,0:T(8,128)}, u32[]{:S(2)}) copy-start(f32[1,8,8,128]{3,2,1,0:T(8,128)} %copy-done.18) | copy-start | bytes 98308
  125.1 13.6 %copy-start.31 = (f32[1,8,8,128]{3,2,1,0:T(8,128)S(1)}, f32[1,8,8,128]{3,2,1,0:T(8,128)}, u32[]{:S(2)}) copy-start(f32[1,8,8,128]{3,2,1,0:T(8,128)} %copy-done.30) | copy-start | bytes 98308
  125.1 13.1 %collective-permute-start.23 = (f32[19,1,10,130]{3,2,1,0:T(8,128)S(1)}, f32[19,1,10,130]{3,2,1,0:T(8,128)S(1)}, u32[]{:S(2)}, u32[]{:S(2)}) collective-permute-start(f32[19,1,10,130]{3,2,1,0:T(8,128)S(1)} %get-tuple-element.130), channel_id=1, source_target_pairs={{1,0},{0,1},{3,2},{2,3},{5,4},{4,5},{7,6},{6,7},{9,8},{8,9},{11,10... | collective-permute-start | bytes 296408 | tf_op jit(solution)/shard_map/ppermute | solution.py:44
  138.5 1.8 copy-start.36
  138.5 1.8 copy-start.37
  138.5 1.8 copy-start.38
  138.5 1.8 copy-start.39
  138.5 1.8 copy-start.40
  139.5 2.4 %copy-start.52 = (f32[1,8,8,128]{3,2,1,0:T(8,128)}, f32[1,8,8,128]{3,2,1,0:T(8,128)S(1)}, u32[]{:S(2)}) copy-start(f32[1,8,8,128]{3,2,1,0:T(8,128)S(1)} %get-tuple-element.51) | copy-start | bytes 98308
  139.5 2.4 %copy-start.53 = (f32[1,8,8,128]{3,2,1,0:T(8,128)}, f32[1,8,8,128]{3,2,1,0:T(8,128)S(1)}, u32[]{:S(2)}) copy-start(f32[1,8,8,128]{3,2,1,0:T(8,128)S(1)} %get-tuple-element.52) | copy-start | bytes 98308
  (32 other events, 39.4 us)
where the time goes:
time: 193 us; the launch traced here: 192 us
  waiting for transfers between devices  79.2 us (41%)
  blocking collectives  40.1 us (21%)
  starting transfers between devices  25.2 us (13%)
  local copies, waits for them, and re-layouts  23.9 us (12%)
  other arithmetic  13.1 us (7%)
  between operations  9.95 us (5%)
    ppermute x12, waiting for transfers between devices, extended(): before = lax.ppermute(last, axis, up)  41.7 us
    psum x1, blocking collectives, per_device(): lax.psum((local_terms[0], local_terms[1], local_terms[2], local_terms[3],...  40.1 us
    ppermute x12, waiting for transfers between devices, extended(): after = lax.ppermute(first, axis, down)  37.6 us
    ppermute x12, starting transfers between devices, extended(): after = lax.ppermute(first, axis, down)  16.9 us
    ppermute x12, starting transfers between devices, extended(): before = lax.ppermute(last, axis, up)  8.35 us
    ppermute x4, local copies, waits for them, and re-layouts, extended(): after = lax.ppermute(first, axis, down)  6.25 us
    unnamed x90, other arithmetic  5.58 us
    ppermute x4, local copies, waits for them, and re-layouts, extended(): before = lax.ppermute(last, axis, up)  5.46 us
  transfers between devices with their start and end apart: 24, of which 22 were waited for; matrix products, arithmetic and copies ran while one was open for 4% of the time, Pallas kernels for 0%

commit v1 on v0

v1 whole, which is shorter than its diff:
```python
import functools

import jax
import jax.numpy as jnp
from jax import lax
from jax.experimental import pallas as pl
from jax.experimental.pallas import tpu as pltpu
from jax.sharding import PartitionSpec as P

STEPS = 4
JUMP = 2
MESH = pl.DeviceIdType.MESH

lattice = [
    (0, 0, 0),
    (1, 0, 0),
    (-1, 0, 0),
    (0, 1, 0),
    (0, -1, 0),
    (0, 0, 1),
    (0, 0, -1),
    (1, 1, 0),
    (-1, -1, 0),
    (1, -1, 0),
    (-1, 1, 0),
    (1, 0, 1),
    (-1, 0, -1),
    (1, 0, -1),
    (-1, 0, 1),
    (0, 1, 1),
    (0, -1, -1),
    (0, 1, -1),
    (0, -1, 1),
]
weights = [1.0 / 3.0] + [1.0 / 18.0] * 6 + [1.0 / 36.0] * 12
limiter = 25.0

slots = [
    (1, 0, -1),
    (1, 0, 0),
    (1, 1, 0),
    (1, -1, 0),
    (1, 0, 1),
    (0, 0, 1),
    (0, 1, 1),
    (0, -1, 1),
    (-1, 0, 1),
    (-1, 0, 0),
    (-1, 1, 0),
    (-1, -1, 0),
    (-1, 0, -1),
    (0, 0, -1),
    (0, 1, -1),
    (0, -1, -1),
    (1, 0, -1),
    (0, 1, 0),
    (0, -1, 0),
    (0, 0, 0),
]
slot_of = {c: i for i, c in enumerate(slots)}
x_first = {1: 0, -1: 8}
z_first = {1: 4, -1: 12}
y_pops = [c for c in lattice if c[1] == 1] + [c for c in lattice if c[1] == -1]
xz_edges = [(1, 0, 1), (-1, 0, 1), (-1, 0, -1), (1, 0, -1)]
xy_edges = [(1, 1, 0), (1, -1, 0), (-1, 1, 0), (-1, -1, 0)]
yz_edges = [(0, 1, 1), (0, -1, 1), (0, 1, -1), (0, -1, -1)]
pairs = [(i, i + 1) for i in range(1, 19, 2)]


def side(sign):
    return 0 if sign == 1 else 1


def moments(f):
    plus = {i: f[i] + f[j] for i, j in pairs}
    minus = {i: f[i] - f[j] for i, j in pairs}
    rho = f[0]
    for i, _ in pairs:
        rho = rho + plus[i]
    comps = []
    for axis in range(3):
        total = None
        for i, _ in pairs:
            c = lattice[i][axis]
            if c:
                term = minus[i]
                total = term * c if total is None else (total + term if c > 0 else total - term)
        comps.append(total)
    return rho, comps


def equilibrium(rho, mom, scale):
    inv = 1.0 / jnp.maximum(rho, 0.5)
    vel = [m * inv for m in mom]
    square = vel[0] * vel[0] + vel[1] * vel[1] + vel[2] * vel[2]
    base = 1.0 - 1.5 * square
    amount = rho if scale is None else scale * rho
    heavy = {w: amount * w for w in sorted(set(weights))}
    rows = [None] * 19
    rows[0] = heavy[weights[0]] * base
    for i, j in pairs:
        proj = None
        for c, v in zip(lattice[i], vel):
            if c:
                proj = (v if c > 0 else -v) if proj is None else (proj + v if c > 0 else proj - v)
        w = heavy[weights[i]]
        even = w * (base + 4.5 * (proj * proj))
        odd = w * (3.0 * proj)
        rows[i] = even + odd
        rows[j] = even - odd
    return rows


def burst_kernel(
    sizes,
    f_hbm,
    omega_hbm,
    obstacle_hbm,
    state_ref,
    diag_ref,
    f_in,
    om_in,
    ob_in,
    post,
    x_send,
    x_recv,
    e_send,
    e_recv,
    c_send,
    c_recv,
    cz_recv,
    moment_a,
    moment_b,
    gathered,
    row_send,
    in_sems,
    send_sems,
    recv_sems,
    sum_send_sems,
    sum_recv_sems,
):
    nx, ny, nz = sizes
    total_devices = nx * ny * nz
    _, Z, X, Y = f_in.shape
    R = X + 16
    gx, gy, gz = (lax.axis_index("gx"), lax.axis_index("gy"), lax.axis_index("gz"))
    me = (gx * ny + gy) * nz + gz

    loads = [
        pltpu.make_async_copy(f_hbm, f_in, in_sems.at[0]),
        pltpu.make_async_copy(omega_hbm, om_in, in_sems.at[1]),
        pltpu.make_async_copy(obstacle_hbm, ob_in, in_sems.at[2]),
    ]
    for load in loads:
        load.start()

    def coords(linear):
        return {"gx": linear // (ny * nz), "gy": (linear // nz) % ny, "gz": linear % nz}

    barrier = pltpu.get_barrier_semaphore()

    def greet(n, carry):
        pl.semaphore_signal(
            barrier, inc=1, device_id=coords((me + n) % total_devices), device_id_type=MESH
        )
        return carry

    lax.fori_loop(1, total_devices, greet, 0)

    lane = lax.broadcasted_iota(jnp.int32, (X, Y), 1)

    def at(z):
        return (z + 1) * R + 8

    def neighbour(offset):
        dx, dy, dz = offset
        return {"gx": (gx + dx + nx) % nx, "gy": (gy + dy + ny) % ny, "gz": (gz + dz + nz) % nz}

    both_z_same = nz == 2

    def messages(s):
        found = []
        for sign in (1, -1):
            rows = pl.ds(at(Z - 1 if sign == 1 else 0), X)
            halo = pl.ds(at(-1 if sign == 1 else Z), X)
            face = pl.ds(z_first[sign], 5)
            found.append((post.at[s, face, rows], post.at[s, face, halo], (0, 0, sign)))
        for sign in (1, -1):
            found.append((x_send.at[s, side(sign)], x_recv.at[s, side(sign)], (sign, 0, 0)))
        for e, c in enumerate(xz_edges):
            found.append((e_send.at[s, e], e_recv.at[s, e], c))
        for sign in (1, -1):
            found.append((c_send.at[s], c_recv.at[s, side(sign), pl.ds(8, X)], (0, sign, 0)))
        for e, c in enumerate(xy_edges):
            row = 4 + side(c[0])
            found.append((e_send.at[s, row], e_recv.at[s, 4 + e], c))
        for e, c in enumerate(yz_edges):
            if both_z_same and c[2] == -1:
                continue
            found.append((c_send.at[s], cz_recv.at[s, e], c))
        return found

    def copies(s):
        return [
            pltpu.make_async_remote_copy(
                src_ref=src,
                dst_ref=dst,
                send_sem=send_sems.at[s, i],
                recv_sem=recv_sems.at[s, i],
                device_id=neighbour(offset),
                device_id_type=MESH,
            )
            for i, (src, dst, offset) in enumerate(messages(s))
        ]

    def collide_plane(s, z, f, packed):
        rho, mom = moments(f)
        for q, value in enumerate([rho] + mom):
            moment_a[q, z] = value
        omega = om_in[z]
        solid = ob_in[z] == 1
        keep = 1.0 - omega
        feq = equilibrium(rho, mom, omega)
        out = {}
        out[0] = jnp.where(solid, f[0], keep * f[0] + feq[0])
        for i, j in pairs:
            out[i] = jnp.where(solid, f[j], keep * f[i] + feq[i])
            out[j] = jnp.where(solid, f[i], keep * f[j] + feq[j])
        by_c = {lattice[i]: out[i] for i in range(19)}
        for k, c in enumerate(slots):
            post[s, k, at(z) : at(z) + X, :] = by_c[c]
        for q, c in enumerate(y_pops):
            k = q * Z + z
            shift = (k + 1) % Y if c[1] == 1 else k
            moved = by_c[c] if shift == 0 else pltpu.roll(by_c[c], shift, 1)
            packed = jnp.where(lane == k, moved, packed)
        return packed

    def send_faces(s, packed):
        for sign in (1, -1):
            row = 8 + (X - 1 if sign == 1 else 0)
            for p in range(5):
                x_send[s, side(sign), p] = post[
                    s, x_first[sign] + p, pl.ds(R + row, Z, stride=R), :
                ]
        for e, (cx, _, cz) in enumerate(xz_edges):
            row = at(Z - 1 if cz == 1 else 0) + (X - 1 if cx == 1 else 0)
            e_send[s, e] = post[s, slot_of[(cx, 0, cz)], pl.ds(row, 1), :]
        c_send[s] = packed
        e_send[s, 4] = packed[X - 1 : X]
        e_send[s, 5] = packed[0:1]
        for copy in copies(s):
            copy.start()

    def receive(s):
        for copy in copies(s):
            copy.wait_recv()
        for sign in (1, -1):
            row = 7 if sign == 1 else X + 8
            for p in range(5):
                post[s, x_first[sign] + p, pl.ds(R + row, Z, stride=R), :] = x_recv[
                    s, side(sign), p
                ]
        for e, (cx, _, cz) in enumerate(xz_edges):
            row = at(-1 if cz == 1 else Z) + (-1 if cx == 1 else X)
            post[s, slot_of[(cx, 0, cz)], pl.ds(row, 1), :] = e_recv[s, e]
        for e, (cx, cy, _) in enumerate(xy_edges):
            row = 7 if cx == 1 else X + 8
            c_recv[s, side(cy), pl.ds(row, 1), :] = e_recv[s, 4 + e]

    def columns(s):
        got = {}
        for sy in (1, -1):
            for cx in (1, 0, -1):
                got[(cx, sy)] = c_recv[s, side(sy), 8 - cx : 8 - cx + X, :]
        for e, c in enumerate(yz_edges):
            slot = yz_edges.index((0, c[1], 1)) if both_z_same else e
            got[c] = cz_recv[s, slot]
        return got

    def stream_plane(s, z, got):
        f = []
        for c in lattice:
            cx, cy, cz = c
            source = z - cz
            slot = slot_of[c]
            if c == (1, 0, -1):
                slot = 0 if source < Z else 16
            row = at(source) - cx
            value = post[s, slot, row : row + X, :]
            if cy:
                outside = source < 0 or source >= Z
                column = got[c] if outside else got[(cx, cy)]
                k = y_pops.index(c) * Z + source % Z
                edge = 0 if cy == 1 else Y - 1
                shift = (edge - k) % Y
                column = column if shift == 0 else pltpu.roll(column, shift, 1)
                value = jnp.where(lane == edge, column, pltpu.roll(value, cy % Y, 1))
            f.append(value)
        return f

    for load in loads:
        load.wait()
    packed = jnp.zeros((X, Y), jnp.float32)
    for z in range(Z):
        packed = collide_plane(0, z, [f_in[i, z] for i in range(19)], packed)
    pl.semaphore_wait(barrier, total_devices - 1)
    send_faces(0, packed)

    def step(s, carry):
        receive(s - 1)
        got = columns(s - 1)
        packed = jnp.zeros((X, Y), jnp.float32)
        for z in range(Z):
            packed = collide_plane(s, z, stream_plane(s - 1, z, got), packed)
        send_faces(s, packed)
        return carry

    lax.fori_loop(1, STEPS, step, 0)
    receive(STEPS - 1)
    got = columns(STEPS - 1)
    sums = [jnp.zeros((X, Y), jnp.float32)] * 10
    for z in range(Z):
        rho, mom = moments(stream_plane(STEPS - 1, z, got))
        now = [rho] + mom
        diff = [now[q] - moment_a[q, z] for q in range(4)]
        for q in range(4):
            moment_b[q, z] = now[q]
            moment_a[q, z] = diff[q]
        terms = [
            diff[0] * diff[0],
            diff[1] * diff[1] + diff[2] * diff[2] + diff[3] * diff[3],
            now[1],
            now[2],
            now[3],
            diff[1],
            diff[2],
            diff[3],
            now[1] * now[1] + now[2] * now[2] + now[3] * now[3],
            now[1] * diff[1] + now[2] * diff[2] + now[3] * diff[3],
        ]
        sums = [a + b for a, b in zip(sums, terms)]

    lane1 = lax.broadcasted_iota(jnp.int32, (1, Y), 1)
    row = jnp.zeros((1, Y), jnp.float32)
    for q, value in enumerate(sums):
        value = jnp.sum(jnp.sum(value, axis=0, keepdims=True), axis=1, keepdims=True)
        row = jnp.where(lane1 == q, value, row)
    row_send[...] = row
    gathered[me] = row

    def share(target, slot):
        return pltpu.make_async_remote_copy(
            src_ref=row_send,
            dst_ref=gathered.at[slot],
            send_sem=sum_send_sems.at[target],
            recv_sem=sum_recv_sems.at[slot],
            device_id=coords(target),
            device_id_type=MESH,
        )

    def share_start(n, carry):
        share((me + n) % total_devices, me).start()
        return carry

    def share_wait(n, carry):
        other = (me + n) % total_devices
        share(other, other).wait_recv()
        return carry

    def share_sent(n, carry):
        share((me + n) % total_devices, me).wait_send()
        return carry

    def steps_sent(s, carry):
        for copy in copies(s):
            copy.wait_send()
        return carry

    lax.fori_loop(1, total_devices, share_start, 0)
    lax.fori_loop(0, STEPS, steps_sent, 0)
    lax.fori_loop(1, total_devices, share_wait, 0)
    total = gathered[0]
    for n in range(1, total_devices):
        total = total + gathered[n]
    lax.fori_loop(1, total_devices, share_sent, 0)

    cells = float(Z * X * Y * total_devices)
    pick = [total[:, q : q + 1] for q in range(10)]
    change = (pick[0] + pick[1]) / cells
    gain = JUMP / (1.0 + limiter * change)
    energy = pick[8] + 2.0 * gain * pick[9] + gain * gain * pick[1]
    diag = [change] + [(pick[2 + a] + gain * pick[5 + a]) / cells for a in range(3)]
    diag.append(energy / cells)
    out = jnp.zeros((1, Y), jnp.float32)
    for q, value in enumerate(diag):
        out = jnp.where(lane1 == q, value, out)
    diag_ref[...] = out
    gains = jnp.broadcast_to(gain, (X, Y))
    for q in range(4):
        for z in range(Z):
            state_ref[q, z] = moment_b[q, z] + gains * moment_a[q, z]


def lift_kernel(state_ref, diag_in, lifted_ref, diag_ref):
    for z in range(state_ref.shape[1]):
        rows = equilibrium(state_ref[0, z], [state_ref[q, z] for q in (1, 2, 3)], None)
        for i in range(19):
            lifted_ref[i, z] = rows[i]
    diag_ref[...] = diag_in[:, 0:5]


def per_device(sizes, populations, omega, obstacle):
    _, Z, X, Y = populations.shape
    R = X + 16
    count = sizes[0] * sizes[1] * sizes[2]
    f32 = jnp.float32
    vmem = pl.BlockSpec(memory_space=pltpu.VMEM)
    hbm = pl.BlockSpec(memory_space=pl.ANY)
    made = 18 if sizes[2] != 2 else 16
    dma = pltpu.SemaphoreType.DMA
    state, diag = pl.pallas_call(
        functools.partial(burst_kernel, sizes),
        out_shape=(
            jax.ShapeDtypeStruct((4, Z, X, Y), f32),
            jax.ShapeDtypeStruct((1, Y), f32),
        ),
        in_specs=[hbm] * 3,
        out_specs=(vmem, vmem),
        scratch_shapes=[
            pltpu.VMEM((19, Z, X, Y), f32),
            pltpu.VMEM((Z, X, Y), f32),
            pltpu.VMEM((Z, X, Y), jnp.int32),
            pltpu.VMEM((STEPS, 20, (Z + 2) * R, Y), f32),
            pltpu.VMEM((STEPS, 2, 5, Z, Y), f32),
            pltpu.VMEM((STEPS, 2, 5, Z, Y), f32),
            pltpu.VMEM((STEPS, 6, 1, Y), f32),
            pltpu.VMEM((STEPS, 8, 1, Y), f32),
            pltpu.VMEM((STEPS, X, Y), f32),
            pltpu.VMEM((STEPS, 2, R, Y), f32),
            pltpu.VMEM((STEPS, 4, X, Y), f32),
            pltpu.VMEM((4, Z, X, Y), f32),
            pltpu.VMEM((4, Z, X, Y), f32),
            pltpu.VMEM((count, 1, Y), f32),
            pltpu.VMEM((1, Y), f32),
            dma((3,)),
            dma((STEPS, made)),
            dma((STEPS, made)),
            dma((count,)),
            dma((count,)),
        ],
        compiler_params=pltpu.CompilerParams(collective_id=0, has_side_effects=True),
    )(populations, omega, obstacle)
    lifted, diag = pl.pallas_call(
        lift_kernel,
        out_shape=(
            jax.ShapeDtypeStruct((19, Z, X, Y), f32),
            jax.ShapeDtypeStruct((1, 5), f32),
        ),
        in_specs=[vmem, vmem],
        out_specs=(vmem, vmem),
    )(state, diag)
    return lifted, diag.reshape(5)


def solution(mesh):
    in_specs = (P(None, "gz", "gx", "gy"), P("gz", "gx", "gy"), P("gz", "gx", "gy"))
    out_specs = (P(None, "gz", "gx", "gy"), P())
    sizes = (mesh.shape["gx"], mesh.shape["gy"], mesh.shape["gz"])
    return jax.shard_map(
        functools.partial(per_device, sizes),
        mesh=mesh,
        in_specs=in_specs,
        out_specs=out_specs,
        check_vma=False,
    )
```

time: 193 us -> 37.8 us (0.20)
  waiting for transfers between devices: 79.2 us -> 0 us
  blocking collectives: 40.1 us -> 0 us
  Pallas kernels: 0 us -> 37 us
  starting transfers between devices: 25.2 us -> 0 us
  local copies, waits for them, and re-layouts: 23.9 us -> 0 us
  other arithmetic: 13.1 us -> 0 us
  between operations: 9.95 us -> 0.64 us
    ppermute x24 -> x0, waiting for transfers between devices: 79.2 us -> none  [the longest x12 41.7 us: extended(): before = lax.ppermute(last, axis, up)]
    psum x1 -> x0, blocking collectives: 40.1 us -> none  [per_device(): lax.psum((local_terms[0], local_terms[1], local_terms[2], local_terms[3],...]
    pallas_call x0 -> x2, Pallas kernels: none -> 37 us  [the longest x1 35.1 us: per_device(): pl.pallas_call(functools.partial(burst_kernel, sizes), out_shape=(jax.Sha...]
    ppermute x24 -> x0, starting transfers between devices: 25.2 us -> none  [the longest x12 16.9 us: extended(): after = lax.ppermute(first, axis, down)]
    ppermute x8 -> x0, local copies, waits for them, and re-layouts: 11.7 us -> none  [the longest x4 6.25 us: extended(): after = lax.ppermute(first, axis, down)]
    slice x16 -> x0, local copies, waits for them, and re-layouts: 8.32 us -> none  [the longest x10 4.99 us: extended(): last = lax.slice_in_dim(x, length - width, length, axis=dim)]
    unnamed x90 -> x0, other arithmetic: 5.58 us -> none
    reduce_sum x3 -> x0, other arithmetic: 3.35 us -> none  [the longest x1 1.5 us: per_device(): jnp.sum(diff_rho * diff_rho)]
  transfers between devices with their start and end apart: 24 -> 0, of which waited for: 22 -> 0; matrix products, arithmetic and copies ran while one was open for 4% -> 0% of each run, Pallas kernels for 0% -> 0%
where the time goes in v1:
time: 37.8 us; the launch traced here: 37.6 us
  Pallas kernels  37 us (98%)
  between operations  0.64 us (2%)
    pallas_call x1, Pallas kernels, per_device(): pl.pallas_call(functools.partial(burst_kernel, sizes), out_shape=(jax.Sha...  35.1 us
    pallas_call x1, Pallas kernels, per_device(): pl.pallas_call(lift_kernel, out_shape=(jax.ShapeDtypeStruct((19, Z, X, Y)...  1.86 us

profile of v1, /device:TPU:0, one launch (start us, length us, event | category | flops | bytes accessed | tf_op | source)
XLA Modules:
  0.0 37.6 jit_solution(11257811402695544344)
XLA Ops:
  0.6 35.1 %shard_map.50 = (f32[4,8,8,128]{3,2,1,0:T(8,128)}, f32[1,128]{1,0:T(1,128)}) custom-call(f32[19,8,8,128]{3,2,1,0:T(8,128)} %f_hbm.1, f32[8,8,128]{2,1,0:T(8,128)} %omega_hbm.1, s32[8,8,128]{2,1,0:T(8,128)} %obstacle_hbm.1), custom_call_target="tpu_custom_call" | custom-call | tf_op jit(solution)/shard_map/pallas_call | solution.py:422
  35.8 1.9 %shard_map.51 = (f32[19,8,8,128]{3,2,1,0:T(8,128)}, f32[1,5]{1,0:T(1,128)}) custom-call(f32[4,8,8,128]{3,2,1,0:T(8,128)} %get-tuple-element.6.state_ref, f32[1,128]{1,0:T(1,128)} %get-tuple-element.7.diag_in), custom_call_target="tpu_custom_call" | custom-call | tf_op jit(solution)/shard_map/pallas_call | solution.py:454
